TPU v7x, 32 devices: a whole 2x2x4 slice. The times are simulated.
32 devices in a mesh: dp: 2 (over x), ep: 16 (over z, y, core).
Axes of the slice: x: 2, y: 2, z: 4, core: 2. Of those that a mesh axis runs over, the one named last changes fastest.
Arguments:
- tokens: bfloat16 [256, 3584], P(('dp', 'ep')), may hold values from -6 to 6
- expert_ids: int32 [2, 256, 8], P(None, ('dp', 'ep')), may hold values from 0 to 15, all different within a row; in each aligned block of 8 rows (0 to 7, 8 to 15, ..., all dimensions but the last counted through in order) at most 6 rows name the same one
- quant_gates: int32 [2, 256, 8], P(None, ('dp', 'ep')), may hold values from 1 to 63
- w_gate: bfloat16 [2, 16, 3584, 1024], P(None, 'ep', None, 'dp'), may hold values from -0.09375 to 0.09375
- w_up: bfloat16 [2, 16, 3584, 1024], P(None, 'ep', None, 'dp'), may hold values from -0.09375 to 0.09375
- w_down: bfloat16 [2, 16, 1024, 3584], P(None, 'ep', 'dp'), may hold values from -0.1875 to 0.1875
Outputs:
- stream_out: bfloat16 [256, 3584], P(('dp', 'ep'))
- expert_load: int32 [2, 16], replicated
Inputs may be any that keep to these rules, and one draw needn't show every extreme that they name: `expert_ids`: in each layer, the 8 tokens of one device name any one expert at most 6 times, a bound that some block reaches.
All inputs are finite; a program needn't handle non-finite values.
Results may differ from a plain program's by a relative error of at most 0.015.
Values may be sent and summed in bfloat16 or wider, within the bound.
A program may use at most 64 MiB of HBM per device.

v0:
```python
import jax
import jax.numpy as jnp
from jax import lax
from jax.sharding import PartitionSpec as P

ROUTE_SCALE = 2.827
EPS = 1e-06


def slot_tables(ids, quant, experts, capacity):
    count_tok, top = ids.shape
    flat = ids.reshape(count_tok * top)
    expert_iota = lax.broadcasted_iota(jnp.int32, (count_tok * top, experts), 1)
    onehot = (flat[:, None] == expert_iota).astype(jnp.int32)
    earlier = jnp.cumsum(onehot, axis=0) - onehot
    position = jnp.sum(earlier * onehot, axis=1)
    target = flat * capacity + position
    slot_iota = lax.broadcasted_iota(jnp.int32, (count_tok * top, experts * capacity), 1)
    picked = target[:, None] == slot_iota
    quant_wide = quant.astype(jnp.float32)
    gates = (ROUTE_SCALE * quant_wide / jnp.sum(quant_wide, axis=1, keepdims=True)).reshape(
        count_tok * top
    )
    spread = jnp.sum(
        jnp.where(picked, gates[:, None], 0.0).reshape(count_tok, top, experts * capacity), axis=1
    )
    chosen = jnp.sum(picked.astype(jnp.float32).reshape(count_tok, top, experts * capacity), axis=1)
    counts = jnp.sum(onehot, axis=0)
    return (chosen, spread, counts)


def per_device(tokens, expert_ids, quant_gates, w_gate, w_up, w_down):
    layers, count_tok, top = expert_ids.shape
    n_ep = lax.axis_size("ep")
    capacity = min(count_tok, max(2, 3 * count_tok * top // (2 * n_ep)))
    width = tokens.shape[1]
    state = tokens
    table = jnp.stack(
        [
            slot_tables(expert_ids[layer], quant_gates[layer], n_ep, capacity)[2]
            for layer in range(layers)
        ]
    )
    loads = lax.psum(table, ("dp", "ep"))
    for layer in range(layers):
        chosen, spread, counts = slot_tables(expert_ids[layer], quant_gates[layer], n_ep, capacity)
        wide = state.astype(jnp.float32)
        normed = (wide * lax.rsqrt(jnp.mean(wide * wide, axis=1, keepdims=True) + EPS)).astype(
            jnp.bfloat16
        )
        outgoing = jnp.dot(
            chosen.T.astype(jnp.bfloat16), normed, preferred_element_type=jnp.float32
        ).astype(jnp.bfloat16)
        arrived = lax.all_to_all(
            outgoing.reshape(n_ep, capacity, width), "ep", split_axis=0, concat_axis=0, tiled=True
        )
        arrived = arrived.reshape(n_ep * capacity, width)
        weight_gate = w_gate[layer, 0]
        weight_up = w_up[layer, 0]
        weight_down = w_down[layer, 0]
        piece = lax.all_gather(arrived, "dp", axis=0, tiled=True)
        gate = jnp.dot(piece, weight_gate, preferred_element_type=jnp.float32)
        upper = jnp.dot(piece, weight_up, preferred_element_type=jnp.float32)
        hidden = (jax.nn.silu(gate) * upper).astype(jnp.bfloat16)
        partial_out = jnp.dot(hidden, weight_down, preferred_element_type=jnp.float32)
        parts = partial_out.astype(jnp.bfloat16)
        summed = lax.psum_scatter(
            parts.astype(jnp.float32).astype(jnp.bfloat16), "dp", scatter_dimension=0, tiled=True
        ).astype(jnp.float32)
        returned = lax.all_to_all(
            summed.reshape(n_ep, capacity, width).astype(jnp.bfloat16),
            "ep",
            split_axis=0,
            concat_axis=0,
            tiled=True,
        ).astype(jnp.float32)
        branch = jnp.dot(
            spread,
            returned.reshape(n_ep * capacity, width),
            precision=lax.Precision.HIGHEST,
            preferred_element_type=jnp.float32,
        )
        state = (state.astype(jnp.float32) + branch).astype(jnp.bfloat16)
    return (state, loads)


def solution(mesh):
    return jax.shard_map(
        per_device,
        mesh=mesh,
        in_specs=(
            P(("dp", "ep"), None),
            P(None, ("dp", "ep"), None),
            P(None, ("dp", "ep"), None),
            P(None, "ep", None, "dp"),
            P(None, "ep", None, "dp"),
            P(None, "ep", "dp", None),
        ),
        out_specs=(P(("dp", "ep"), None), P()),
        check_vma=False,
    )
```

profile of v0, /device:TPU:0, one launch (start us, length us, event | category | flops | bytes accessed | tf_op | source)
XLA Modules:
  0.0 278.6 jit_solution(12670127936095068034)
XLA Ops:
  7.2 0.0 all-gather.3.cloned.1.call-start
  7.2 1.0 fusion.47
  8.2 0.9 convert_reduce_fusion.2
  9.0 0.7 fusion.60
  9.7 0.1 eq.53
  9.8 0.1 eq.48
  9.9 0.1 fusion.53
  10.0 0.1 reduce_window_sum.17
  10.1 0.2 fusion.54
  10.3 0.1 reduce_sum.113
  10.4 0.1 fusion.52
  10.4 0.1 reduce_window_sum.18
  10.5 0.2 fusion.55
  10.7 0.1 reduce_sum.119
  10.8 0.8 bitcast_divide_fusion
  11.6 0.7 bitcast_add_fusion
  12.3 0.1 convert_reduce_fusion.1
  12.4 1.2 convolution_convert_fusion.3
  13.6 0.2 reshape.136
  13.9 29.6 %all_to_all.20 = bf16[16,6,3584]{2,1,0:T(8,128)(2,1)S(1)} all-to-all(bf16[16,6,3584]{2,1,0:T(8,128)(2,1)S(1)} %reshape.136), channel_id=1, replica_groups=mesh['dp'=2,'ep'=16] {'ep'}, dimensions={0} | all-to-all | bytes 1376256 | tf_op jit(solution)/shard_map/all_to_all | solution.py:54
  43.5 1.1 reshape.137
  44.6 0.0 all-gather.3.cloned.1.call-update
  44.6 0.0 reduce-scatter.3.cloned.1.call-start
  44.7 24.9 %all-gather.3.cloned.1.call-done = bf16[192,3584]{1,0:T(8,128)(2,1)} async-done(((bf16[96,3584]{1,0:T(8,128)(2,1)}), bf16[192,3584]{1,0:T(8,128)(2,1)}) %all-gather.3.cloned.1.call-update) | async-done | bytes 1376272 | tf_op jit(solution)/shard_map/all_gather | solution.py:61
  69.6 3.4 %fusion.11 = f32[192,512]{1,0:T(8,128)S(1)} fusion(bf16[192,3584]{1,0:T(8,128)(2,1)} %all-gather.3.cloned.1.call-done, bf16[2,1,3584,512]{3,2,1,0:T(8,128)(2,1)} %param.9), kind=kOutput, calls=%fused_computation.17 | convolution fusion | flops 704643072 | bytes 5439488 | tf_op jit(solution)/shard_map/dot_general | solution.py:62
  73.0 5.9 %convolution_convert_fusion.1 = bf16[192,3584]{1,0:T(8,128)(2,1)} fusion(bf16[2,1,512,3584]{3,2,1,0:T(8,128)(2,1)} %param.11, bf16[192,3584]{1,0:T(8,128)(2,1)S(1)} %copy-done.1, bf16[2,1,3584,512]{3,2,1,0:T(8,128)(2,1)} %param.10, f32[192,512]{1,0:T(8,128)S(1)} %fusion.11), kind=kOutput, calls=%fused_computation.1 | convolution fusion | flops 1410564096 | bytes 10485760 | tf_op jit(solution)/shard_map/dot_general | solution.py:65
  79.0 24.1 %reduce-scatter.3.cloned.1.call-done = bf16[96,3584]{1,0:T(8,128)(2,1)} async-done(((bf16[192,3584]{1,0:T(8,128)(2,1)}), bf16[96,3584]{1,0:T(8,128)(2,1)}) %reduce-scatter.3.cloned.1.call-update) | async-done | bytes 688144 | tf_op jit(solution)/shard_map/reduce_scatter | solution.py:67
  103.2 2.1 convert_element_type.103
  105.3 5.6 %all-to-all-start.1 = ((bf16[16,6,3584]{2,1,0:T(8,128)(2,1)}), bf16[16,6,3584]{2,1,0:T(8,128)(2,1)S(1)}, u32[]{:S(2)}, u32[]{:S(2)}) async-start(bf16[16,6,3584]{2,1,0:T(8,128)(2,1)} %convert_element_type.103), calls=%async_computation.2 | async-start | bytes 1835008 | tf_op jit(solution)/shard_map/all_to_all | solution.py:70
  110.9 0.0 all-gather.5.cloned.1.call-start
  111.0 0.1 convert_reduce_fusion
  111.1 20.6 %all-to-all-done.1 = bf16[16,6,3584]{2,1,0:T(8,128)(2,1)S(1)} async-done(((bf16[16,6,3584]{2,1,0:T(8,128)(2,1)}), bf16[16,6,3584]{2,1,0:T(8,128)(2,1)S(1)}, u32[]{:S(2)}, u32[]{:S(2)}) %all-to-all-start.1) | async-done | bytes 688160 | tf_op jit(solution)/shard_map/all_to_all | solution.py:70
  131.7 0.2 reshape.138
  132.0 0.5 multiply_reduce_fusion
  132.5 0.4 convolution_convert_fusion.2
  132.9 0.2 reshape.139
  133.1 28.3 %all_to_all.21 = bf16[16,6,3584]{2,1,0:T(8,128)(2,1)S(1)} all-to-all(bf16[16,6,3584]{2,1,0:T(8,128)(2,1)S(1)} %reshape.139), channel_id=1, replica_groups=mesh['dp'=2,'ep'=16] {'ep'}, dimensions={0} | all-to-all | bytes 1376256 | tf_op jit(solution)/shard_map/all_to_all | solution.py:54
  161.4 1.1 reshape.140
  162.5 0.0 reduce-scatter.5.cloned.1.call-start
  162.6 24.0 %all-gather.5.cloned.1.call-done = bf16[192,3584]{1,0:T(8,128)(2,1)} async-done(((bf16[96,3584]{1,0:T(8,128)(2,1)}), bf16[192,3584]{1,0:T(8,128)(2,1)}) %all-gather.5.cloned.1.call-update) | async-done | bytes 1376272 | tf_op jit(solution)/shard_map/all_gather | solution.py:61
  186.6 3.4 %fusion.6 = f32[192,512]{1,0:T(8,128)S(1)} fusion(bf16[192,3584]{1,0:T(8,128)(2,1)} %all-gather.5.cloned.1.call-done, bf16[2,1,3584,512]{3,2,1,0:T(8,128)(2,1)} %param.9), kind=kOutput, calls=%fused_computation.12 | convolution fusion | flops 704643072 | bytes 5439488 | tf_op jit(solution)/shard_map/dot_general | solution.py:62
  190.0 5.9 %convolution_convert_fusion = bf16[192,3584]{1,0:T(8,128)(2,1)} fusion(bf16[2,1,512,3584]{3,2,1,0:T(8,128)(2,1)} %param.11, bf16[192,3584]{1,0:T(8,128)(2,1)S(1)} %copy-done.2, bf16[2,1,3584,512]{3,2,1,0:T(8,128)(2,1)} %param.10, f32[192,512]{1,0:T(8,128)S(1)} %fusion.6), kind=kOutput, calls=%fused_computation | convolution fusion | flops 1410564096 | bytes 10485760 | tf_op jit(solution)/shard_map/dot_general | solution.py:65
  196.0 24.1 %reduce-scatter.5.cloned.1.call-done = bf16[96,3584]{1,0:T(8,128)(2,1)} async-done(((bf16[192,3584]{1,0:T(8,128)(2,1)}), bf16[96,3584]{1,0:T(8,128)(2,1)}) %reduce-scatter.5.cloned.1.call-update) | async-done | bytes 688144 | tf_op jit(solution)/shard_map/reduce_scatter | solution.py:67
  220.1 2.1 convert_element_type.114
  222.3 5.6 %all-to-all-start.3 = ((bf16[16,6,3584]{2,1,0:T(8,128)(2,1)}), bf16[16,6,3584]{2,1,0:T(8,128)(2,1)S(1)}, u32[]{:S(2)}, u32[]{:S(2)}) async-start(bf16[16,6,3584]{2,1,0:T(8,128)(2,1)} %convert_element_type.114), calls=%async_computation.5 | async-start | bytes 1835008 | tf_op jit(solution)/shard_map/all_to_all | solution.py:70
  227.9 42.9 %psum.7 = s32[2,16]{1,0:T(2,128)} all-reduce(s32[2,16]{1,0:T(2,128)S(1)} %pad_add_fusion), channel_id=1, replica_groups=mesh['dp'=2,'ep'=16] {'dp','ep'}, use_global_device_ids=true, to_apply=%region_16.17 | all-reduce | flops 32 | bytes 256 | tf_op jit(solution)/shard_map/psum | solution.py:44
  270.9 0.2 reshape.141
  271.1 1.0 fusion.2
  (13 shorter events, 0.1 us)
Async XLA Ops:
  7.2 62.4 %all-gather.3.cloned.1.call-start = ((), (), s32[]{:S(2)}) async-start(), calls=%async_computation.6 | async-start | bytes 2064384 | tf_op jit(solution)/shard_map/all_gather | solution.py:61
  44.6 58.5 %reduce-scatter.3.cloned.1.call-start = ((), (), s32[]{:S(2)}) async-start(), calls=%async_computation.7 | async-start | bytes 2064384 | tf_op jit(solution)/shard_map/reduce_scatter | solution.py:67
  69.6 3.4 %copy-start.1 = (bf16[192,3584]{1,0:T(8,128)(2,1)S(1)}, bf16[192,3584]{1,0:T(8,128)(2,1)}, u32[]{:S(2)}) copy-start(bf16[192,3584]{1,0:T(8,128)(2,1)} %all-gather.3.cloned.1.call-done) | copy-start | bytes 4128772
  79.0 53.0 %copy-start = (bf16[8,3584]{1,0:T(8,128)(2,1)S(1)}, bf16[8,3584]{1,0:T(8,128)(2,1)}, u32[]{:S(2)}) copy-start(bf16[8,3584]{1,0:T(8,128)(2,1)} %param.6) | copy-start | bytes 172036
  105.3 26.4 %all-to-all-start.1 = ((bf16[16,6,3584]{2,1,0:T(8,128)(2,1)}), bf16[16,6,3584]{2,1,0:T(8,128)(2,1)S(1)}, u32[]{:S(2)}, u32[]{:S(2)}) async-start(bf16[16,6,3584]{2,1,0:T(8,128)(2,1)} %convert_element_type.103), calls=%async_computation.2 | async-start | bytes 1835008 | tf_op jit(solution)/shard_map/all_to_all | solution.py:70
  110.9 75.7 %all-gather.5.cloned.1.call-start = ((), (), s32[]{:S(2)}) async-start(), calls=%async_computation.8 | async-start | bytes 2064384 | tf_op jit(solution)/shard_map/all_gather | solution.py:61
  162.5 57.6 %reduce-scatter.5.cloned.1.call-start = ((), (), s32[]{:S(2)}) async-start(), calls=%async_computation.9 | async-start | bytes 2064384 | tf_op jit(solution)/shard_map/reduce_scatter | solution.py:67
  186.6 3.4 %copy-start.2 = (bf16[192,3584]{1,0:T(8,128)(2,1)S(1)}, bf16[192,3584]{1,0:T(8,128)(2,1)}, u32[]{:S(2)}) copy-start(bf16[192,3584]{1,0:T(8,128)(2,1)} %all-gather.5.cloned.1.call-done) | copy-start | bytes 4128772
  222.3 48.6 %all-to-all-start.3 = ((bf16[16,6,3584]{2,1,0:T(8,128)(2,1)}), bf16[16,6,3584]{2,1,0:T(8,128)(2,1)S(1)}, u32[]{:S(2)}, u32[]{:S(2)}) async-start(bf16[16,6,3584]{2,1,0:T(8,128)(2,1)} %convert_element_type.114), calls=%async_computation.5 | async-start | bytes 1835008 | tf_op jit(solution)/shard_map/all_to_all | solution.py:70
Sparse Core Ops, SparseCore 0:
  44.7 24.8 all-gather.2
  79.1 23.9 reduce-scatter.2
  162.7 23.8 all-gather.4
  196.1 23.9 reduce-scatter.4
where the time goes:
time: 279 us
  waiting for transfers between devices  118 us (42%)
  blocking collectives  101 us (36%)
  matrix products  21.8 us (8%)
  between operations  13.9 us (5%)
  starting transfers between devices  11.4 us (4%)
  local copies, waits for them, and re-layouts  8.5 us (3%)
  other arithmetic  4.25 us (2%)
    all_to_all x2, blocking collectives, per_device(): lax.all_to_all(outgoing.reshape(n_ep, capacity, width), 'ep', split_axis=...  57.9 us
    all_gather x2, waiting for transfers between devices, per_device(): piece = lax.all_gather(arrived, 'dp', axis=0, tiled=True)  48.9 us
    reduce_scatter x2, waiting for transfers between devices, per_device(): lax.psum_scatter(parts.astype(jnp.float32).astype(jnp.bfloat16), 'dp', sc...  48.3 us
    psum x1, blocking collectives, per_device(): loads = lax.psum(table, ('dp', 'ep'))  42.9 us
    all_to_all x2, waiting for transfers between devices, per_device(): lax.all_to_all(summed.reshape(n_ep, capacity, width).astype(jnp.bfloat16)...  20.6 us
    dot_general x2, matrix products, per_device(): jnp.dot(hidden, weight_down, preferred_element_type=jnp.float32)  11.9 us
    all_to_all x2, starting transfers between devices, per_device(): lax.all_to_all(summed.reshape(n_ep, capacity, width).astype(jnp.bfloat16)...  11.2 us
    dot_general x2, matrix products, per_device(): gate = jnp.dot(piece, weight_gate, preferred_element_type=jnp.float32)  6.86 us
  transfers between devices with their start and end apart: 6, of which 5 were waited for; matrix products, arithmetic and copies ran while one was open for 0% of the time, Pallas kernels for 0%

commit v1 on v0

--- a/solution.py
+++ b/solution.py
@@ -5,6 +5,9 @@
 
 ROUTE_SCALE = 2.827
 EPS = 1e-06
+choose_the_frame = lambda my_tile, axis_name, which_axis: lax.psum(
+    lax.psum(my_tile, axis_name), which_axis
+)
 
 
 def slot_tables(ids, quant, experts, capacity):
@@ -41,7 +44,7 @@
             for layer in range(layers)
         ]
     )
-    loads = lax.psum(table, ("dp", "ep"))
+    loads = choose_the_frame(table, "ep", "dp")
     for layer in range(layers):
         chosen, spread, counts = slot_tables(expert_ids[layer], quant_gates[layer], n_ep, capacity)
         wide = state.astype(jnp.float32)

time: 279 us -> 265 us (0.950)
  blocking collectives: 101 us -> 86.6 us
    psum x1 -> x2, blocking collectives: 42.9 us -> 28.7 us  [the longest x1 23.9 us: lax.psum(my_tile, axis_name)]
where the time goes in v1:
time: 265 us; the launch traced here: 264 us
  waiting for transfers between devices  118 us (45%)
  blocking collectives  86.6 us (33%)
  matrix products  21.8 us (8%)
  between operations  13.9 us (5%)
  starting transfers between devices  11.4 us (4%)
  local copies, waits for them, and re-layouts  8.5 us (3%)
  other arithmetic  4.25 us (2%)
    all_to_all x2, blocking collectives, per_device(): lax.all_to_all(outgoing.reshape(n_ep, capacity, width), 'ep', split_axis=...  57.9 us
    all_gather x2, waiting for transfers between devices, per_device(): piece = lax.all_gather(arrived, 'dp', axis=0, tiled=True)  48.9 us
    reduce_scatter x2, waiting for transfers between devices, per_device(): lax.psum_scatter(parts.astype(jnp.float32).astype(jnp.bfloat16), 'dp', sc...  48.3 us
    psum x1, blocking collectives, lax.psum(my_tile, axis_name)  23.9 us
    all_to_all x2, waiting for transfers between devices, per_device(): lax.all_to_all(summed.reshape(n_ep, capacity, width).astype(jnp.bfloat16)...  20.6 us
    dot_general x2, matrix products, per_device(): jnp.dot(hidden, weight_down, preferred_element_type=jnp.float32)  11.9 us
    all_to_all x2, starting transfers between devices, per_device(): lax.all_to_all(summed.reshape(n_ep, capacity, width).astype(jnp.bfloat16)...  11.2 us
    dot_general x2, matrix products, per_device(): gate = jnp.dot(piece, weight_gate, preferred_element_type=jnp.float32)  6.86 us
  transfers between devices with their start and end apart: 6, of which 5 were waited for; matrix products, arithmetic and copies ran while one was open for 0% of the time, Pallas kernels for 0%

profile of v1, /device:TPU:0, one launch (start us, length us, event | category | flops | bytes accessed | tf_op | source)
XLA Modules:
  0.0 264.4 jit_solution(4663025497791743629)
XLA Ops:
  7.2 0.0 all-gather.3.cloned.1.call-start
  7.2 1.0 fusion.47
  8.2 0.9 convert_reduce_fusion.2
  9.0 0.7 fusion.60
  9.7 0.1 eq.53
  9.8 0.1 eq.48
  9.9 0.1 fusion.53
  10.0 0.1 reduce_window_sum.17
  10.1 0.2 fusion.54
  10.3 0.1 reduce_sum.113
  10.4 0.1 fusion.52
  10.4 0.1 reduce_window_sum.18
  10.5 0.2 fusion.55
  10.7 0.1 reduce_sum.119
  10.8 0.8 bitcast_divide_fusion
  11.6 0.7 bitcast_add_fusion
  12.3 0.1 convert_reduce_fusion.1
  12.4 1.2 convolution_convert_fusion.3
  13.6 0.2 reshape.136
  13.9 29.6 %all_to_all.20 = bf16[16,6,3584]{2,1,0:T(8,128)(2,1)S(1)} all-to-all(bf16[16,6,3584]{2,1,0:T(8,128)(2,1)S(1)} %reshape.136), channel_id=1, replica_groups=mesh['dp'=2,'ep'=16] {'ep'}, dimensions={0} | all-to-all | bytes 1376256 | tf_op jit(solution)/shard_map/all_to_all | solution.py:57
  43.5 1.1 reshape.137
  44.6 0.0 reduce-scatter.3.cloned.1.call-start
  44.7 24.9 %all-gather.3.cloned.1.call-done = bf16[192,3584]{1,0:T(8,128)(2,1)} async-done(((bf16[96,3584]{1,0:T(8,128)(2,1)}), bf16[192,3584]{1,0:T(8,128)(2,1)}) %all-gather.3.cloned.1.call-update) | async-done | bytes 1376272 | tf_op jit(solution)/shard_map/all_gather | solution.py:64
  69.6 3.4 %fusion.11 = f32[192,512]{1,0:T(8,128)S(1)} fusion(bf16[192,3584]{1,0:T(8,128)(2,1)} %all-gather.3.cloned.1.call-done, bf16[2,1,3584,512]{3,2,1,0:T(8,128)(2,1)} %param.9), kind=kOutput, calls=%fused_computation.17 | convolution fusion | flops 704643072 | bytes 5439488 | tf_op jit(solution)/shard_map/dot_general | solution.py:65
  73.0 5.9 %convolution_convert_fusion.1 = bf16[192,3584]{1,0:T(8,128)(2,1)} fusion(bf16[2,1,512,3584]{3,2,1,0:T(8,128)(2,1)} %param.11, bf16[192,3584]{1,0:T(8,128)(2,1)S(1)} %copy-done.1, bf16[2,1,3584,512]{3,2,1,0:T(8,128)(2,1)} %param.10, f32[192,512]{1,0:T(8,128)S(1)} %fusion.11), kind=kOutput, calls=%fused_computation.1 | convolution fusion | flops 1410564096 | bytes 10485760 | tf_op jit(solution)/shard_map/dot_general | solution.py:68
  79.0 24.1 %reduce-scatter.3.cloned.1.call-done = bf16[96,3584]{1,0:T(8,128)(2,1)} async-done(((bf16[192,3584]{1,0:T(8,128)(2,1)}), bf16[96,3584]{1,0:T(8,128)(2,1)}) %reduce-scatter.3.cloned.1.call-update) | async-done | bytes 688144 | tf_op jit(solution)/shard_map/reduce_scatter | solution.py:70
  103.2 2.1 convert_element_type.103
  105.3 5.6 %all-to-all-start.1 = ((bf16[16,6,3584]{2,1,0:T(8,128)(2,1)}), bf16[16,6,3584]{2,1,0:T(8,128)(2,1)S(1)}, u32[]{:S(2)}, u32[]{:S(2)}) async-start(bf16[16,6,3584]{2,1,0:T(8,128)(2,1)} %convert_element_type.103), calls=%async_computation.2 | async-start | bytes 1835008 | tf_op jit(solution)/shard_map/all_to_all | solution.py:73
  110.9 0.0 all-gather.5.cloned.1.call-start
  111.0 0.1 convert_reduce_fusion
  111.1 20.6 %all-to-all-done.1 = bf16[16,6,3584]{2,1,0:T(8,128)(2,1)S(1)} async-done(((bf16[16,6,3584]{2,1,0:T(8,128)(2,1)}), bf16[16,6,3584]{2,1,0:T(8,128)(2,1)S(1)}, u32[]{:S(2)}, u32[]{:S(2)}) %all-to-all-start.1) | async-done | bytes 688160 | tf_op jit(solution)/shard_map/all_to_all | solution.py:73
  131.7 0.2 reshape.138
  132.0 0.5 multiply_reduce_fusion
  132.5 0.4 convolution_convert_fusion.2
  132.9 0.2 reshape.139
  133.1 28.3 %all_to_all.21 = bf16[16,6,3584]{2,1,0:T(8,128)(2,1)S(1)} all-to-all(bf16[16,6,3584]{2,1,0:T(8,128)(2,1)S(1)} %reshape.139), channel_id=1, replica_groups=mesh['dp'=2,'ep'=16] {'ep'}, dimensions={0} | all-to-all | bytes 1376256 | tf_op jit(solution)/shard_map/all_to_all | solution.py:57
  161.4 1.1 reshape.140
  162.5 0.0 reduce-scatter.5.cloned.1.call-start
  162.6 24.0 %all-gather.5.cloned.1.call-done = bf16[192,3584]{1,0:T(8,128)(2,1)} async-done(((bf16[96,3584]{1,0:T(8,128)(2,1)}), bf16[192,3584]{1,0:T(8,128)(2,1)}) %all-gather.5.cloned.1.call-update) | async-done | bytes 1376272 | tf_op jit(solution)/shard_map/all_gather | solution.py:64
  186.6 3.4 %fusion.6 = f32[192,512]{1,0:T(8,128)S(1)} fusion(bf16[192,3584]{1,0:T(8,128)(2,1)} %all-gather.5.cloned.1.call-done, bf16[2,1,3584,512]{3,2,1,0:T(8,128)(2,1)} %param.9), kind=kOutput, calls=%fused_computation.12 | convolution fusion | flops 704643072 | bytes 5439488 | tf_op jit(solution)/shard_map/dot_general | solution.py:65
  190.0 5.9 %convolution_convert_fusion = bf16[192,3584]{1,0:T(8,128)(2,1)} fusion(bf16[2,1,512,3584]{3,2,1,0:T(8,128)(2,1)} %param.11, bf16[192,3584]{1,0:T(8,128)(2,1)S(1)} %copy-done.2, bf16[2,1,3584,512]{3,2,1,0:T(8,128)(2,1)} %param.10, f32[192,512]{1,0:T(8,128)S(1)} %fusion.6), kind=kOutput, calls=%fused_computation | convolution fusion | flops 1410564096 | bytes 10485760 | tf_op jit(solution)/shard_map/dot_general | solution.py:68
  196.0 24.1 %reduce-scatter.5.cloned.1.call-done = bf16[96,3584]{1,0:T(8,128)(2,1)} async-done(((bf16[192,3584]{1,0:T(8,128)(2,1)}), bf16[96,3584]{1,0:T(8,128)(2,1)}) %reduce-scatter.5.cloned.1.call-update) | async-done | bytes 688144 | tf_op jit(solution)/shard_map/reduce_scatter | solution.py:70
  220.1 2.1 convert_element_type.114
  222.3 5.6 %all-to-all-start.3 = ((bf16[16,6,3584]{2,1,0:T(8,128)(2,1)}), bf16[16,6,3584]{2,1,0:T(8,128)(2,1)S(1)}, u32[]{:S(2)}, u32[]{:S(2)}) async-start(bf16[16,6,3584]{2,1,0:T(8,128)(2,1)} %convert_element_type.114), calls=%async_computation.5 | async-start | bytes 1835008 | tf_op jit(solution)/shard_map/all_to_all | solution.py:73
  227.9 23.9 %psum.14 = s32[2,16]{1,0:T(2,128)S(1)} all-reduce(s32[2,16]{1,0:T(2,128)S(1)} %pad_add_fusion), channel_id=1, replica_groups=mesh['dp'=2,'ep'=16] {'ep'}, use_global_device_ids=true, to_apply=%region_16.17 | all-reduce | flops 32 | bytes 256 | tf_op jit(solution)/shard_map/psum | solution.py:9
  251.8 4.8 %psum.15 = s32[2,16]{1,0:T(2,128)} all-reduce(s32[2,16]{1,0:T(2,128)S(1)} %psum.14), channel_id=1, replica_groups=mesh['dp'=2,'ep'=16] {'dp'}, use_global_device_ids=true, to_apply=%region_17.18 | all-reduce | flops 32 | bytes 256 | tf_op jit(solution)/shard_map/psum | solution.py:8
  256.6 0.2 reshape.141
  256.8 1.0 fusion.2
  (14 shorter events, 0.1 us)
Async XLA Ops:
  7.2 62.4 %all-gather.3.cloned.1.call-start = ((), (), s32[]{:S(2)}) async-start(), calls=%async_computation.6 | async-start | bytes 2064384 | tf_op jit(solution)/shard_map/all_gather | solution.py:64
  44.6 58.5 %reduce-scatter.3.cloned.1.call-start = ((), (), s32[]{:S(2)}) async-start(), calls=%async_computation.7 | async-start | bytes 2064384 | tf_op jit(solution)/shard_map/reduce_scatter | solution.py:70
  69.6 3.4 %copy-start.1 = (bf16[192,3584]{1,0:T(8,128)(2,1)S(1)}, bf16[192,3584]{1,0:T(8,128)(2,1)}, u32[]{:S(2)}) copy-start(bf16[192,3584]{1,0:T(8,128)(2,1)} %all-gather.3.cloned.1.call-done) | copy-start | bytes 4128772
  79.0 53.0 %copy-start = (bf16[8,3584]{1,0:T(8,128)(2,1)S(1)}, bf16[8,3584]{1,0:T(8,128)(2,1)}, u32[]{:S(2)}) copy-start(bf16[8,3584]{1,0:T(8,128)(2,1)} %param.6) | copy-start | bytes 172036
  105.3 26.4 %all-to-all-start.1 = ((bf16[16,6,3584]{2,1,0:T(8,128)(2,1)}), bf16[16,6,3584]{2,1,0:T(8,128)(2,1)S(1)}, u32[]{:S(2)}, u32[]{:S(2)}) async-start(bf16[16,6,3584]{2,1,0:T(8,128)(2,1)} %convert_element_type.103), calls=%async_computation.2 | async-start | bytes 1835008 | tf_op jit(solution)/shard_map/all_to_all | solution.py:73
  110.9 75.7 %all-gather.5.cloned.1.call-start = ((), (), s32[]{:S(2)}) async-start(), calls=%async_computation.8 | async-start | bytes 2064384 | tf_op jit(solution)/shard_map/all_gather | solution.py:64
  162.5 57.6 %reduce-scatter.5.cloned.1.call-start = ((), (), s32[]{:S(2)}) async-start(), calls=%async_computation.9 | async-start | bytes 2064384 | tf_op jit(solution)/shard_map/reduce_scatter | solution.py:70
  186.6 3.4 %copy-start.2 = (bf16[192,3584]{1,0:T(8,128)(2,1)S(1)}, bf16[192,3584]{1,0:T(8,128)(2,1)}, u32[]{:S(2)}) copy-start(bf16[192,3584]{1,0:T(8,128)(2,1)} %all-gather.5.cloned.1.call-done) | copy-start | bytes 4128772
  222.3 34.3 %all-to-all-start.3 = ((bf16[16,6,3584]{2,1,0:T(8,128)(2,1)}), bf16[16,6,3584]{2,1,0:T(8,128)(2,1)S(1)}, u32[]{:S(2)}, u32[]{:S(2)}) async-start(bf16[16,6,3584]{2,1,0:T(8,128)(2,1)} %convert_element_type.114), calls=%async_computation.5 | async-start | bytes 1835008 | tf_op jit(solution)/shard_map/all_to_all | solution.py:73
Sparse Core Ops, SparseCore 0:
  44.7 24.8 all-gather.2
  79.1 23.9 reduce-scatter.2
  162.7 23.8 all-gather.4
  196.1 23.9 reduce-scatter.4
